TPU v7x, 32 devices: a whole 2x2x4 slice. The times are simulated.
32 devices in a mesh: dp: 4 (over z), expert: 4 (over y, x), tensor: 2 (over core).
Axes of the slice: x: 2, y: 2, z: 4, core: 2. Of those that a mesh axis runs over, the one named last changes fastest.
Arguments:
- tokens: bfloat16 [512, 6144], P('dp', 'tensor'), may hold values from -6 to 6
- out_grad: bfloat16 [512, 6144], P('dp', 'tensor'), may hold values from -6 to 6
- router_weight: bfloat16 [6144, 4], P('tensor'), may hold values from -0.078125 to 0.078125
- gate_weight: bfloat16 [4, 6144, 8192], P('expert', 'tensor', 'dp'), may hold values from -0.078125 to 0.078125
- up_weight: bfloat16 [4, 6144, 8192], P('expert', 'tensor', 'dp'), may hold values from -0.078125 to 0.078125
- down_weight: bfloat16 [4, 8192, 6144], P('expert', 'dp', 'tensor'), may hold values from -0.0625 to 0.0625
- expert_index: int32 [512, 2], P('dp'), may hold values from 0 to 3, as said below
- slot_index: int32 [512, 2], P('dp'), may hold values from 0 to 95, as said below
Outputs:
- tokens_grad: bfloat16 [512, 6144], P(('dp', 'expert'), 'tensor')
- router_grad: float32 [6144, 4], P('tensor')
- gate_grad: bfloat16 [4, 6144, 8192], P('expert', 'tensor', 'dp')
- up_grad: bfloat16 [4, 6144, 8192], P('expert', 'tensor', 'dp')
- down_grad: bfloat16 [4, 8192, 6144], P('expert', 'dp', 'tensor')
Inputs may be any that keep to these rules, and one draw needn't show every extreme that they name: `expert_index`: each row names two different experts; in each aligned block of 128 rows no expert is named more than 96 times, and one expert is named exactly 96 times in every block. `slot_index`: entry k of a row is a slot of the expert in entry k of the same row of expert_index; within one aligned block of 128 rows the choices of one expert have distinct slots.
All inputs are finite; a program needn't handle non-finite values.
Results may differ from a plain program's by a relative error of at most 0.025.
Values may be sent and summed in bfloat16 or wider, within the bound.
A program may use at most 128 MiB of HBM per device.

v0:
```python
import functools

import jax
import jax.numpy as jnp
from jax import lax
from jax.experimental import pallas as pl
from jax.experimental.pallas import tpu as pltpu
from jax.sharding import PartitionSpec as P

CAP = 96
F32 = jnp.float32
BF16 = jnp.bfloat16
LANES = 128
MESH = pl.DeviceIdType.MESH
VMEM_LIMIT = 67_043_328


def dot_nn(a, b):
    return lax.dot_general(a, b, (((1,), (0,)), ((), ())), preferred_element_type=F32)


def dot_nt(a, b):
    return lax.dot_general(a, b, (((1,), (1,)), ((), ())), preferred_element_type=F32)


def dot_tn(a, b):
    return lax.dot_general(a, b, (((0,), (0,)), ((), ())), preferred_element_type=F32)


def sigmoid(x):
    return 1.0 / (1.0 + jnp.exp(-x))


def three_pieces(x):
    high = x.astype(BF16).astype(F32)
    rest = x - high
    middle = rest.astype(BF16).astype(F32)
    return high, middle, rest - middle


def split_count(width, most):
    for count in range(most, 0, -1):
        if width % (count * LANES) == 0:
            return count
    return 1


def layer_kernel(
    n_dp, n_exp, n_ten, f_chunks, w_chunks,
    tokens, out_grad, router, index, gate_w, up_w, down_w,
    hidden_out, gg_out, gu_out, st_out, sg_out, dx_out, rg_out,
    gw, uw, db, tok, gra, st, sg, own, peer, tdx, ax, ay, bsend, brecv, csend, crecv, acc,
    idx, rw, logit_own, logit_peer, prob, sel, selt, spb, dacc,
    dsend, dz, d1, dx1, d2, dx2, lgr, term,
    load_sem, in_sem, idx_ss, idx_rs, z_ss, z_rs, p_ss, p_rs, r_ss, r_rs,
    t_ss, t_rs, lg_ss, lg_rs, a_ss, a_rs, b_ss, b_rs, c_ss, c_rs, dz_ss, dz_rs, de_ss, de_rs, out_sem,
):
    d = lax.axis_index("dp")
    e = lax.axis_index("expert")
    t = lax.axis_index("tensor")
    quarter, width = tok.shape[2], tok.shape[3]
    rows = n_exp * quarter
    half = quarter // 2
    hidden_w = gw.shape[1]
    fc = hidden_w // f_chunks
    wc = width // w_chunks
    x_id, y_id, far = e ^ 1, e ^ 2, e ^ 3

    def at_dp(k):
        return (lax.rem(d + k, n_dp), e, t)

    def at_exp(which):
        return (d, which, t)

    def at_ten(k):
        return (d, e, lax.rem(t + k, n_ten))

    def block_from(k):
        return lax.rem(d - k + n_dp, n_dp)

    def remote(src, dst, ss, rs, device):
        return pltpu.make_async_remote_copy(
            src_ref=src, dst_ref=dst, send_sem=ss, recv_sem=rs, device_id=device, device_id_type=MESH
        )

    shifts = []
    for k in range(1, n_dp // 2 + 1):
        shifts.append(k)
        if n_dp - k != k:
            shifts.append(n_dp - k)

    idx_load = pltpu.make_async_copy(index, idx.at[d], load_sem.at[0])
    rw_load = pltpu.make_async_copy(router, rw, load_sem.at[1])
    gw_load = pltpu.make_async_copy(gate_w, gw, load_sem.at[2])
    uw_load = pltpu.make_async_copy(up_w, uw, load_sem.at[3])
    ins = (tokens, out_grad)
    bufs = (tok, gra)
    slots = (st, sg)
    in_load = [pltpu.make_async_copy(ins[a], bufs[a].at[d], in_sem.at[a]) for a in range(2)]
    down_load = [
        pltpu.make_async_copy(down_w.at[pl.ds(j * fc, fc)], db.at[j % 2], load_sem.at[4 + j])
        for j in range(f_chunks)
    ]
    idx_load.start()
    in_load[0].start()
    in_load[1].start()
    rw_load.start()

    barrier = pltpu.get_barrier_semaphore()
    others = [at_dp(k) for k in range(1, n_dp)] + [at_exp(x_id), at_exp(y_id)]
    others += [at_ten(k) for k in range(1, n_ten)]
    for device in others:
        pl.semaphore_signal(barrier, inc=1, device_id=device, device_id_type=MESH)
    pl.semaphore_wait(barrier, len(others))

    def idx_copy(k):
        return remote(idx.at[d], idx.at[d], idx_ss.at[k - 1], idx_rs.at[k - 1], at_dp(k))

    def idx_arrival(k):
        b = block_from(k)
        return remote(idx.at[b], idx.at[b], idx_ss.at[k - 1], idx_rs.at[k - 1], at_dp(k))

    def z_copy(a, k):
        return remote(
            ins[a].at[e], bufs[a].at[d, e], z_ss.at[a, k - 1], z_rs.at[a, k - 1], at_dp(k)
        )

    def z_arrival(a, k):
        b = block_from(k)
        return remote(
            bufs[a].at[b, e], bufs[a].at[b, e], z_ss.at[a, k - 1], z_rs.at[a, k - 1], at_dp(k)
        )

    def plane_copy(a, k, side, quarter_id):
        b = block_from(k)
        ref = bufs[a].at[b, quarter_id]
        return remote(
            ref, ref, p_ss.at[a, k - 1, side], p_rs.at[a, k - 1, side], at_exp((x_id, y_id)[side])
        )

    def relay_copy(a, k, side, quarter_id):
        b = block_from(k)
        ref = bufs[a].at[b, quarter_id, pl.ds((1 - side) * half, half)]
        return remote(
            ref, ref, r_ss.at[a, k - 1, side], r_rs.at[a, k - 1, side], at_exp((x_id, y_id)[side])
        )

    for k in shifts:
        z_copy(0, k).start()
    idx_load.wait()
    for k in shifts:
        idx_copy(k).start()
    for k in shifts:
        z_copy(1, k).start()
    gw_load.start()
    uw_load.start()
    for j in range(min(2, f_chunks)):
        down_load[j].start()

    order = [(a, k) for a in range(2) for k in shifts]
    n_order = len(order)

    def hop_plane(a, k):
        z_arrival(a, k).wait_recv()
        plane_copy(a, k, 0, e).start()
        plane_copy(a, k, 1, e).start()

    def hop_relay(a, k):
        plane_copy(a, k, 0, x_id).wait_recv()
        relay_copy(a, k, 1, x_id).start()
        plane_copy(a, k, 1, y_id).wait_recv()
        relay_copy(a, k, 0, y_id).start()

    def hop_last(a, k):
        relay_copy(a, k, 0, far).wait_recv()
        relay_copy(a, k, 1, far).wait_recv()

    def to_slots(a, block):
        base = pl.multiple_of(block * CAP, 16)
        lanes = width // split_count(width, 6)

        def body(i, carry):
            cols = pl.ds(pl.multiple_of(i * lanes, LANES), lanes)
            values = bufs[a][block, :, :, cols].reshape(rows, lanes)
            slots[a][pl.ds(base, CAP), cols] = dot_nn(sel[block, :CAP], values).astype(BF16)
            return carry

        lax.fori_loop(0, width // lanes, body, 0)

    def make_select(block):
        pos = lax.broadcasted_iota(jnp.int32, (LANES, rows), 0)
        first = (idx[block, 0:1] == e) & (idx[block, 2:3] == pos)
        second = (idx[block, 1:2] == e) & (idx[block, 3:4] == pos)
        hot = jnp.where(first | second, 1.0, 0.0).astype(F32)
        sel[block] = hot.astype(BF16)
        selt[block] = hot.T.astype(BF16)

    def part_matmul(which, j):
        weight = (gw, uw)[which]
        cols = pl.ds(j * fc, fc)
        tile = fc // split_count(fc, 2)

        def body(i, carry):
            sub = pl.ds(pl.multiple_of(j * fc + i * tile, LANES), tile)
            own[which, :, sub] = dot_nn(st[...], weight[:, sub]).astype(BF16)
            return carry

        lax.fori_loop(0, fc // tile, body, 0)
        send_part(which, j)

    def part_copy(which, j, k):
        cols = pl.ds(j * fc, fc)
        return remote(
            own.at[which, :, cols],
            peer.at[k - 1, which, :, cols],
            t_ss.at[k - 1, which, j],
            t_rs.at[k - 1, which, j],
            at_ten(k),
        )

    def send_part(which, j):
        for k in range(1, n_ten):
            part_copy(which, j, k).start()

    def logits_of(block):
        logit_own[block] = dot_nt(rw[...], tok[block].reshape(rows, width))

    def logit_copy(k):
        return remote(
            logit_own, logit_peer.at[k - 1], lg_ss.at[k - 1], lg_rs.at[k - 1], at_ten(k)
        )

    work = [functools.partial(part_matmul, w, j) for w in range(2) for j in range(f_chunks)]
    done_tokens = False
    made = set()
    spread = n_order + 2 - (len(shifts) + 1)

    def own_block(a):
        in_load[a].wait()
        to_slots(a, d)

    for step in range(n_order + 2):
        if step < n_order:
            hop_plane(*order[step])
        if step == 0:
            rw_load.wait()
            make_select(d)
            own_block(0)
            logits_of(d)
        if 0 <= step - 1 < n_order:
            hop_relay(*order[step - 1])
        if 0 <= step - 2 < n_order:
            a, k = order[step - 2]
            hop_last(a, k)
            block = block_from(k)
            if a == 0:
                idx_arrival(k).wait_recv()
                make_select(block)
                logits_of(block)
            to_slots(a, block)
            if a == 0 and k == shifts[-1]:
                done_tokens = True
                for m in range(1, n_ten):
                    logit_copy(m).start()
                gw_load.wait()
                uw_load.wait()
        if step == len(shifts) + 1:
            own_block(1)
        if done_tokens:
            left = n_order + 2 - step
            share = -(-len(work) // left)
            for piece in work[:share]:
                piece()
            work = work[share:]
    for piece in work:
        piece()

    for k in shifts:
        idx_copy(k).wait_send()
    for a, k in order:
        z_copy(a, k).wait_send()
        for side in range(2):
            plane_copy(a, k, side, e).wait_send()
            relay_copy(a, k, 1 - side, (x_id, y_id)[side]).wait_send()

    for m in range(1, n_ten):
        logit_copy(m).wait()
    choice = lax.broadcasted_iota(jnp.int32, (8, rows), 0)
    for r in range(n_dp):
        logits = logit_own[r]
        for m in range(1, n_ten):
            logits = logits + logit_peer[m - 1, r]
        chosen = [
            jnp.sum(jnp.where(choice == idx[r, k : k + 1], logits, 0.0), axis=0, keepdims=True)
            for k in range(2)
        ]
        p0 = sigmoid(chosen[0] - chosen[1])
        p1 = sigmoid(chosen[1] - chosen[0])
        prob[r, 0:1] = p0
        prob[r, 1:2] = p1
        pos = lax.broadcasted_iota(jnp.int32, (CAP, rows), 0)
        first = (idx[r, 0:1] == e) & (idx[r, 2:3] == pos)
        second = (idx[r, 1:2] == e) & (idx[r, 3:4] == pos)
        low0 = p0.astype(BF16).astype(F32)
        low1 = p1.astype(BF16).astype(F32)
        picked = jnp.where(first, low0, 0.0) + jnp.where(second, low1, 0.0)
        column = jnp.sum(picked, axis=1, keepdims=True)
        spb[pl.ds(r * CAP, CAP)] = jnp.broadcast_to(column, (CAP, LANES))
    dacc[...] = jnp.zeros_like(dacc)

    def mix(j):
        for which in range(3):
            for k in range(1, n_ten):
                part_copy(which, j, k).wait()
        per = fc // LANES

        def body(i, carry):
            r = i // per
            base = pl.ds(pl.multiple_of(r * CAP, 16), CAP)
            cols = pl.ds(pl.multiple_of(j * fc + (i - r * per) * LANES, LANES), LANES)
            total = []
            for which in range(3):
                value = own[which, base, cols].astype(F32)
                for k in range(1, n_ten):
                    value = value + peer[k - 1, which, base, cols].astype(F32)
                total.append(value)
            g, u, ga = total
            s = sigmoid(g)
            gs = g * s
            hid = (gs * u).astype(BF16)
            dacc[base] = dacc[base] + hid.astype(F32) * ga
            act = spb[base] * ga
            own[0, base, cols] = hid
            own[1, base, cols] = (act * u * s * (1.0 + g * (1.0 - s))).astype(BF16)
            own[2, base, cols] = (act * gs).astype(BF16)
            return carry

        lax.fori_loop(0, n_dp * per, body, 0)

    for j in range(f_chunks):
        down_load[j].wait()
        tile = fc // split_count(fc, 2)

        def body(i, carry, j=j, tile=tile):
            sub = pl.ds(pl.multiple_of(j * fc + i * tile, LANES), tile)
            rows_in = pl.ds(pl.multiple_of(i * tile, LANES), tile)
            own[2, :, sub] = dot_nt(sg[...], db[j % 2, rows_in]).astype(BF16)
            return carry

        lax.fori_loop(0, fc // tile, body, 0)
        if j + 2 < f_chunks:
            down_load[j + 2].start()
        send_part(2, j)
        if j >= 1:
            mix(j - 1)
    mix(f_chunks - 1)

    st_store = pltpu.make_async_copy(st, st_out, out_sem.at[3])
    st_store.start()
    own_store = [
        pltpu.make_async_copy(own.at[w], (hidden_out, gg_out, gu_out)[w], out_sem.at[w])
        for w in range(3)
    ]
    for copy in own_store:
        copy.start()

    for r in range(n_dp):
        column = jnp.sum(dacc[pl.ds(r * CAP, CAP)], axis=1, keepdims=True)
        pos = lax.broadcasted_iota(jnp.int32, (CAP, rows), 0)
        for k in range(2):
            hit = (idx[r, k : k + 1] == e) & (idx[r, 2 + k : 3 + k] == pos)
            dsend[pl.ds(2 * r + k, 1)] = jnp.sum(
                jnp.where(hit, column, 0.0), axis=0, keepdims=True
            )

    def dz_copy(k):
        return remote(dsend, dz.at[k - 1], dz_ss.at[k - 1], dz_rs.at[k - 1], at_dp(k))

    def de_copy(side):
        return remote(
            (d1, d2)[side], (dx1, dx2)[side], de_ss.at[side], de_rs.at[side],
            at_exp((x_id, y_id)[side]),
        )

    for k in shifts:
        dz_copy(k).start()

    def scale_grads():
        lanes = width // split_count(width, 6)

        def body(i, carry):
            cols = pl.ds(pl.multiple_of(i * lanes, LANES), lanes)
            for r in range(n_dp):
                base = pl.ds(r * CAP, CAP)
                sg[base, cols] = (spb[base][:, 0:1] * sg[base, cols].astype(F32)).astype(BF16)
            return carry

        lax.fori_loop(0, width // lanes, body, 0)

    def router_one():
        total = dsend[...]
        for k in shifts:
            dz_copy(k).wait()
        for k in shifts:
            total = total + dz[k - 1]
        d1[...] = total
        de_copy(0).start()

    def router_two():
        de_copy(0).wait()
        d2[...] = d1[...] + dx1[...]
        de_copy(1).start()

    def router_three():
        de_copy(1).wait()
        total = d2[...] + dx2[...]
        for r in range(n_dp):
            g0 = total[2 * r : 2 * r + 1]
            g1 = total[2 * r + 1 : 2 * r + 2]
            p0, p1 = prob[r, 0:1], prob[r, 1:2]
            mixed = p0 * g0 + p1 * g1
            w0, w1 = p0 * (g0 - mixed), p1 * (g1 - mixed)
            lg = jnp.where(choice == idx[r, 0:1], w0, 0.0) + jnp.where(
                choice == idx[r, 1:2], w1, 0.0
            )
            for i, piece in enumerate(three_pieces(lg)):
                lgr[r, pl.ds(8 * i, 8)] = piece
        lanes = width // split_count(width, 6)

        def body(i, carry):
            cols = pl.ds(pl.multiple_of(i * lanes, LANES), lanes)
            out = jnp.zeros((24, lanes), F32)
            for r in range(n_dp):
                values = tok[r, :, :, cols].reshape(rows, lanes)
                out = out + dot_nn(lgr[r].astype(BF16), values)
            term[0:8, cols] = out[0:8] + out[8:16] + out[16:24]
            return carry

        lax.fori_loop(0, width // lanes, body, 0)

    def dx_chunk(c):
        tile = wc // split_count(wc, 3)

        def body(i, carry):
            cols = pl.ds(pl.multiple_of(c * wc + i * tile, LANES), tile)
            part = dot_nt(own[1], gw[cols]) + dot_nt(own[2], uw[cols])
            part = part.astype(BF16)
            for r in range(n_dp):
                one = dot_nn(selt[r][:, :CAP], part[r * CAP : (r + 1) * CAP]).astype(BF16)
                tdx[r, :, :, cols] = one.reshape(n_exp, quarter, tile)
            return carry

        lax.fori_loop(0, wc // tile, body, 0)

    def a_copy(c, side, which):
        cols = pl.ds(c * wc, wc)
        quarter_id = ((x_id, far), (y_id, far))[side][which]
        return remote(
            tdx.at[:, quarter_id, pl.ds(side * half, half), cols],
            (ax, ay)[side].at[which, :, :, cols],
            a_ss.at[c, side, which],
            a_rs.at[c, side, which],
            at_exp((x_id, y_id)[side]),
        )

    def b_copy(c, side):
        cols = pl.ds(c * wc, wc)
        return remote(
            bsend.at[side, :, :, cols],
            brecv.at[side, :, :, cols],
            b_ss.at[c, side],
            b_rs.at[c, side],
            at_exp((y_id, x_id)[side]),
        )

    def c_copy(c, k):
        cols = pl.ds(c * wc, wc)
        return remote(
            csend.at[lax.rem(d + k, n_dp), :, cols],
            crecv.at[k - 1, :, cols],
            c_ss.at[c, k - 1],
            c_rs.at[c, k - 1],
            at_dp(k),
        )

    def start_a(c):
        for which in (1, 0):
            for side in range(2):
                a_copy(c, side, which).start()

    def relay_b(c):
        cols = pl.ds(c * wc, wc)
        for side in range(2):
            a_copy(c, side, 1).wait()
            mine = tdx[:, (y_id, x_id)[side], pl.ds(side * half, half), cols].astype(F32)
            got = (ax, ay)[side][1, :, :, cols].astype(F32)
            bsend[side, :, :, cols] = (mine + got).astype(BF16)
            b_copy(c, side).start()

    def cross_c(c):
        cols = pl.ds(c * wc, wc)
        for side in range(2):
            a_copy(c, side, 0).wait()
            b_copy(c, side).wait()
            part = pl.ds(side * half, half)
            total = tdx[:, e, part, cols].astype(F32)
            total = total + (ax, ay)[side][0, :, :, cols].astype(F32)
            total = total + brecv[side, :, :, cols].astype(F32)
            csend[:, part, cols] = total.astype(BF16)
        for k in shifts:
            c_copy(c, k).start()

    def finish(c):
        cols = pl.ds(c * wc, wc)
        total = csend[d, :, cols].astype(F32)
        for k in shifts:
            c_copy(c, k).wait()
        for k in shifts:
            total = total + crecv[k - 1, :, cols].astype(F32)
        acc[:, cols] = total

    small = [router_one, router_two, router_three]
    for c in range(w_chunks + 3):
        if c < w_chunks:
            dx_chunk(c)
            start_a(c)
        if 0 <= c - 1 < w_chunks:
            relay_b(c - 1)
        if 0 <= c - 2 < w_chunks:
            cross_c(c - 2)
        if c == 1:
            scale_grads()
            sg_store = pltpu.make_async_copy(sg, sg_out, out_sem.at[4])
            sg_store.start()
        elif small and c >= 2:
            small.pop(0)()
        if 0 <= c - 3 < w_chunks:
            finish(c - 3)
    for job in small:
        job()

    mine = lgr[d]
    weights = jnp.concatenate([rw[...]] * 3, axis=0)
    whole = dot_tn(mine.astype(BF16), weights)
    logit_term = whole.reshape(n_exp, quarter, width)
    tdx_rows = logit_term
    acc2 = tdx_rows
    term[8:8 + rows] = acc2.reshape(rows, width)
    pick = term[pl.ds(pl.multiple_of(8 + e * quarter, 8), quarter)]
    st_store.wait()
    csend[0] = (acc[...] + pick).astype(BF16)
    dx_store = pltpu.make_async_copy(csend.at[0], dx_out, out_sem.at[5])
    dx_store.start()
    rg_store = pltpu.make_async_copy(term.at[pl.ds(0, 8)], rg_out, out_sem.at[6])
    rg_store.start()
    for copy in own_store:
        copy.wait()
    sg_store.wait()
    dx_store.wait()
    rg_store.wait()


def run_kernel(n_dp, n_exp, n_ten, tokens, out_grad, router_weight, gate_w, up_w, down_w, index):
    rows, width = tokens.shape
    hidden_w = gate_w.shape[1]
    quarter = rows // n_exp
    half = quarter // 2
    slots = n_dp * CAP
    f_chunks = split_count(hidden_w, 4)
    w_chunks = split_count(width, 4)
    fc = hidden_w // f_chunks
    n_choice = router_weight.shape[1]
    router = jnp.pad(router_weight.T, ((0, 8 - n_choice), (0, 0)))
    shape = jax.ShapeDtypeStruct
    any_spec = pl.BlockSpec(memory_space=pl.ANY)
    dma = pltpu.SemaphoreType.DMA
    vmem = pltpu.VMEM
    d_rows = -(-2 * n_dp // 8) * 8
    z = n_dp - 1
    m = max(n_ten - 1, 1)
    scratch = [
        vmem((width, hidden_w), BF16),
        vmem((width, hidden_w), BF16),
        vmem((2, fc, width), BF16),
        vmem((n_dp, n_exp, quarter, width), BF16),
        vmem((n_dp, n_exp, quarter, width), BF16),
        vmem((slots, width), BF16),
        vmem((slots, width), BF16),
        vmem((3, slots, hidden_w), BF16),
        vmem((m, 3, slots, hidden_w), BF16),
        vmem((n_dp, n_exp, quarter, width), BF16),
        vmem((2, n_dp, half, width), BF16),
        vmem((2, n_dp, half, width), BF16),
        vmem((2, n_dp, half, width), BF16),
        vmem((2, n_dp, half, width), BF16),
        vmem((n_dp, quarter, width), BF16),
        vmem((z, quarter, width), BF16),
        vmem((quarter, width), F32),
        vmem((n_dp, 8, rows), jnp.int32),
        vmem((8, width), BF16),
        vmem((n_dp, 8, rows), F32),
        vmem((m, n_dp, 8, rows), F32),
        vmem((n_dp, 8, rows), F32),
        vmem((n_dp, LANES, rows), BF16),
        vmem((n_dp, rows, LANES), BF16),
        vmem((slots, LANES), F32),
        vmem((slots, LANES), F32),
        vmem((d_rows, rows), F32),
        vmem((z, d_rows, rows), F32),
        vmem((d_rows, rows), F32),
        vmem((d_rows, rows), F32),
        vmem((d_rows, rows), F32),
        vmem((d_rows, rows), F32),
        vmem((n_dp, 24, rows), F32),
        vmem((8 + rows, width), F32),
        dma((4 + f_chunks,)),
        dma((2,)),
        dma((z,)), dma((z,)),
        dma((2, z)), dma((2, z)),
        dma((2, z, 2)), dma((2, z, 2)),
        dma((2, z, 2)), dma((2, z, 2)),
        dma((m, 3, f_chunks)), dma((m, 3, f_chunks)),
        dma((m,)), dma((m,)),
        dma((w_chunks, 2, 2)), dma((w_chunks, 2, 2)),
        dma((w_chunks, 2)), dma((w_chunks, 2)),
        dma((w_chunks, z)), dma((w_chunks, z)),
        dma((z,)), dma((z,)),
        dma((2,)), dma((2,)),
        dma((7,)),
    ]
    flops = 2 * slots * width * hidden_w * 5
    return pl.pallas_call(
        functools.partial(layer_kernel, n_dp, n_exp, n_ten, f_chunks, w_chunks),
        out_shape=(
            shape((slots, hidden_w), BF16),
            shape((slots, hidden_w), BF16),
            shape((slots, hidden_w), BF16),
            shape((slots, width), BF16),
            shape((slots, width), BF16),
            shape((quarter, width), BF16),
            shape((8, width), F32),
        ),
        in_specs=[any_spec] * 7,
        out_specs=(any_spec,) * 7,
        scratch_shapes=scratch,
        compiler_params=pltpu.CompilerParams(
            collective_id=0, has_side_effects=True, vmem_limit_bytes=VMEM_LIMIT
        ),
        cost_estimate=pl.CostEstimate(
            flops=flops, bytes_accessed=6 * width * hidden_w, transcendentals=0
        ),
        name="layer",
    )(
        tokens.reshape(n_exp, quarter, width),
        out_grad.reshape(n_exp, quarter, width),
        router, index, gate_w, up_w, down_w,
    )


def build(n_dp, n_exp, n_ten):
    def shards(
        tokens, out_grad, router_weight, gate_weight, up_weight, down_weight, expert_index, slot_index
    ):
        n_choice = router_weight.shape[1]
        index = jnp.concatenate([expert_index, slot_index], axis=1).T
        index = jnp.pad(index, ((0, 4), (0, 0)))
        hidden, grad_gate, grad_up, slot_tokens, scaled, tokens_grad, router_t = run_kernel(
            n_dp, n_exp, n_ten, tokens, out_grad, router_weight,
            gate_weight[0], up_weight[0], down_weight[0], index,
        )
        gate_grad = dot_tn(slot_tokens, grad_gate).astype(BF16)
        up_grad = dot_tn(slot_tokens, grad_up).astype(BF16)
        down_grad = dot_tn(hidden, scaled).astype(BF16)
        router_grad = router_t[:n_choice].T
        return (tokens_grad, router_grad, gate_grad[None], up_grad[None], down_grad[None])

    return shards


def solution(mesh):
    in_specs = (
        P("dp", "tensor"),
        P("dp", "tensor"),
        P("tensor", None),
        P("expert", "tensor", "dp"),
        P("expert", "tensor", "dp"),
        P("expert", "dp", "tensor"),
        P("dp", None),
        P("dp", None),
    )
    out_specs = (
        P(("dp", "expert"), "tensor"),
        P("tensor", None),
        P("expert", "tensor", "dp"),
        P("expert", "tensor", "dp"),
        P("expert", "dp", "tensor"),
    )
    shards = build(mesh.shape["dp"], mesh.shape["expert"], mesh.shape["tensor"])
    return jax.shard_map(shards, mesh=mesh, in_specs=in_specs, out_specs=out_specs, check_vma=False)
```

profile of v0, /device:TPU:0, one launch (start us, length us, event | category | flops | bytes accessed | tf_op | source)
XLA Modules:
  0.0 154.6 jit_solution(1502380621832699094)
XLA Ops:
  0.6 0.7 add_bitcast_fusion
  1.3 0.6 pad.9.index
  1.9 1.4 pad.8.router
  3.3 118.2 %layer.1 = (bf16[384,2048]{1,0:T(8,128)(2,1)}, bf16[384,2048]{1,0:T(8,128)(2,1)}, bf16[384,2048]{1,0:T(8,128)(2,1)}, bf16[384,3072]{1,0:T(8,128)(2,1)}, bf16[384...) custom-call(bf16[4,32,3072]{2,1,0:T(8,128)(2,1)} %bitcast.26, bf16[4,32,3072]{2,1,0:T(8,128)(2,1)} %bitcast.27, ...), custom_call_target="tpu_custom_call" | custom-call | flops 24159191040 | bytes 37748736 | tf_op jit(solution)/shard_map/layer/pallas_call | solution.py:632
  121.5 1.5 slice_bitcast_fusion
  123.0 0.0 copy-start.1
  123.0 0.0 copy-start.3
  123.0 11.6 %convert_bitcast_fusion.2 = bf16[1,3072,2048]{2,1,0:T(8,128)(2,1)} fusion(bf16[384,3072]{1,0:T(8,128)(2,1)} %get-tuple-element.14, bf16[384,2048]{1,0:T(8,128)(2,1)} %get-tuple-element.15), kind=kOutput, calls=%fused_computation.2 | convolution fusion | flops 4838129664 | bytes 16515072 | tf_op jit(solution)/shard_map/dot_general | solution.py:27
  134.6 0.0 copy-done.1
  134.6 0.0 copy-done.3
  134.6 0.0 copy-start.2
  134.6 0.0 copy-start.4
  134.6 9.7 %convert_bitcast_fusion.1 = bf16[1,3072,2048]{2,1,0:T(8,128)(2,1)} fusion(bf16[384,3072]{1,0:T(8,128)(2,1)S(1)} %copy-done.1, bf16[384,2048]{1,0:T(8,128)(2,1)S(1)} %copy-done.3), kind=kOutput, calls=%fused_computation.1 | convolution fusion | flops 4838129664 | bytes 16515072 | tf_op jit(solution)/shard_map/dot_general | solution.py:27
  144.3 0.0 copy-done.2
  144.3 0.0 copy-done.4
  144.3 0.0 copy-start
  144.3 9.7 %convert_bitcast_fusion = bf16[1,2048,3072]{2,1,0:T(8,128)(2,1)} fusion(bf16[384,2048]{1,0:T(8,128)(2,1)S(1)} %copy-done.4, bf16[384,3072]{1,0:T(8,128)(2,1)S(1)} %copy-done.2), kind=kOutput, calls=%fused_computation | convolution fusion | flops 4838129664 | bytes 16515072 | tf_op jit(solution)/shard_map/dot_general | solution.py:27
  154.0 0.0 copy-done
  154.0 0.7 copy.14
Async XLA Ops:
  123.0 11.6 %copy-start.1 = (bf16[384,3072]{1,0:T(8,128)(2,1)S(1)}, bf16[384,3072]{1,0:T(8,128)(2,1)}, u32[]{:S(2)}) copy-start(bf16[384,3072]{1,0:T(8,128)(2,1)} %get-tuple-element.14) | copy-start | bytes 7077892
  123.0 11.6 %copy-start.3 = (bf16[384,2048]{1,0:T(8,128)(2,1)S(1)}, bf16[384,2048]{1,0:T(8,128)(2,1)}, u32[]{:S(2)}) copy-start(bf16[384,2048]{1,0:T(8,128)(2,1)} %get-tuple-element.16) | copy-start | bytes 4718596
  134.6 9.7 %copy-start.2 = (bf16[384,3072]{1,0:T(8,128)(2,1)S(1)}, bf16[384,3072]{1,0:T(8,128)(2,1)}, u32[]{:S(2)}) copy-start(bf16[384,3072]{1,0:T(8,128)(2,1)} %get-tuple-element.18) | copy-start | bytes 7077892
  134.6 9.7 %copy-start.4 = (bf16[384,2048]{1,0:T(8,128)(2,1)S(1)}, bf16[384,2048]{1,0:T(8,128)(2,1)}, u32[]{:S(2)}) copy-start(bf16[384,2048]{1,0:T(8,128)(2,1)} %get-tuple-element.17) | copy-start | bytes 4718596
  144.3 9.7 %copy-start = (bf16[32,3072]{1,0:T(8,128)(2,1)S(1)}, bf16[32,3072]{1,0:T(8,128)(2,1)}, u32[]{:S(2)}) copy-start(bf16[32,3072]{1,0:T(8,128)(2,1)} %get-tuple-element.24) | copy-start | bytes 589828
where the time goes:
time: 155 us
  Pallas kernels  118 us (76%)
  matrix products  30.9 us (20%)
  local copies, waits for them, and re-layouts  4.18 us (3%)
    pallas_call x1, Pallas kernels, run_kernel(): pl.pallas_call(functools.partial(layer_kernel, n_dp, n_exp, n_ten, f_chun...  118 us
    dot_general x3, matrix products, dot_tn(): lax.dot_general(a, b, (((0,), (0,)), ((), ())), preferred_element_type=F32)  30.9 us

commit v1 on v0

v1 whole, which is shorter than its diff:
```python
import functools

import jax
import jax.numpy as jnp
from jax import lax
from jax.experimental import pallas as pl
from jax.experimental.pallas import tpu as pltpu
from jax.sharding import PartitionSpec as P

CAP = 96
LAGS = (1, 2)
LEADS = (0.5, 1.5)
EARLY_EVENTS = 3
F32 = jnp.float32
BF16 = jnp.bfloat16
LANES = 128
MESH = pl.DeviceIdType.MESH
VMEM_LIMIT = 67_043_328


def dot_nn(a, b):
    return lax.dot_general(a, b, (((1,), (0,)), ((), ())), preferred_element_type=F32)


def dot_nt(a, b):
    return lax.dot_general(a, b, (((1,), (1,)), ((), ())), preferred_element_type=F32)


def dot_tn(a, b):
    return lax.dot_general(a, b, (((0,), (0,)), ((), ())), preferred_element_type=F32)


def sigmoid(x):
    return 1.0 / (1.0 + jnp.exp(-x))


def three_pieces(x):
    high = x.astype(BF16).astype(F32)
    rest = x - high
    middle = rest.astype(BF16).astype(F32)
    return high, middle, rest - middle


def split_count(width, most):
    for count in range(most, 0, -1):
        if width % (count * LANES) == 0:
            return count
    return 1


def spare_columns(width):
    return width // 12 if width % (12 * LANES) == 0 else 0


def layer_kernel(
    n_dp, n_exp, n_ten, f_chunks, w_chunks, splits, dg_chunks,
    tokens, out_grad, router, chosen_in, place_in, gate_w, up_w, down_w,
    gg_out, gu_out, st_out, dg_out, dx_out, rg_out,
    gw, uw, dw, tok, gra, st, sg, own, peer, ax, ay, bsend, brecv, csend, crecv, acc,
    pick, place, rw, logit_own, logit_peer, prob, sel, selt, spb, dacc,
    dsend, dz, d1, dx1, d2, dx2, lgr, term, rgt,
    load_sem, in_sem, idx_ss, idx_rs, z_ss, z_rs, p_ss, p_rs, r_ss, r_rs,
    t_ss, t_rs, lg_ss, lg_rs, a_ss, a_rs, b_ss, b_rs, c_ss, c_rs, dz_ss, dz_rs, de_ss, de_rs, out_sem, dg_sem,
):
    d = lax.axis_index("dp")
    e = lax.axis_index("expert")
    t = lax.axis_index("tensor")
    quarter, width = tok.shape[2], tok.shape[3]
    rows = n_exp * quarter
    half = quarter // 2
    n_choice = rw.shape[0]
    hidden_w = gw.shape[1]
    fc = hidden_w // f_chunks
    wc = width // w_chunks
    extra = spare_columns(width)
    piece = (width - extra) // splits
    n_pieces = splits + (1 if extra else 0)
    x_id, y_id, far = e ^ 1, e ^ 2, e ^ 3
    tdx = gra
    last = n_dp - 1
    f_tile = fc // split_count(fc, 2)

    def at_dp(k):
        return (lax.rem(d + k, n_dp), e, t)

    def at_exp(which):
        return (d, which, t)

    def at_ten(k):
        return (d, e, lax.rem(t + k, n_ten))

    def remote(src, dst, ss, rs, device):
        return pltpu.make_async_remote_copy(
            src_ref=src, dst_ref=dst, send_sem=ss, recv_sem=rs, device_id=device, device_id_type=MESH
        )

    short = jnp.minimum(d, last - d)
    blocks, from_left = [d], [None]
    for j in range(last):
        inner = j < 2 * short
        distance = jnp.where(inner, j // 2 + 1, j - short + 1)
        left = jnp.where(inner, 1 - j % 2, jnp.where(2 * d > last, 1, 0))
        blocks.append(d + distance * (1 - 2 * left))
        from_left.append(left)
    shifts = range(1, n_dp)

    ins = (tokens, out_grad)
    bufs = (tok, gra)
    slots = (st, sg)
    load = pltpu.make_async_copy
    idx_load = [
        load(chosen_in, pick.at[d], load_sem.at[0]),
        load(place_in, place.at[d], load_sem.at[1]),
    ]
    rw_load = load(router, rw, load_sem.at[2])
    gw_load = load(gate_w, gw, load_sem.at[3])
    uw_load = load(up_w, uw, load_sem.at[4])
    dw_load = load(down_w, dw, load_sem.at[5])
    in_load = [load(ins[a], bufs[a].at[d], in_sem.at[a]) for a in range(2)]
    for copy in idx_load:
        copy.start()
    in_load[0].start()
    rw_load.start()

    barrier = pltpu.get_barrier_semaphore()
    others = [at_dp(k) for k in shifts] + [at_exp(x_id), at_exp(y_id)]
    others += [at_ten(k) for k in range(1, n_ten)]
    for device in others:
        pl.semaphore_signal(barrier, inc=1, device_id=device, device_id_type=MESH)
    pl.semaphore_wait(barrier, len(others))

    def idx_copy(k, which):
        ref = (pick, place)[which].at[d]
        return remote(ref, ref, idx_ss.at[which, k - 1], idx_rs.at[which, d], at_dp(k))

    def idx_arrival(p, which):
        ref = (pick, place)[which].at[blocks[p]]
        return remote(ref, ref, idx_ss.at[which, 0], idx_rs.at[which, blocks[p]], at_dp(1))

    def line_part(ref, h):
        if h == splits:
            return ref.at[:, :, pl.ds(splits * piece, extra)]
        return ref.at[e, :, pl.ds(h * piece, piece)]

    def z_own(a, h, side):
        other = jnp.minimum(d + 1, last) if side == 0 else jnp.maximum(d - 1, 0)
        return remote(
            line_part(ins[a], h),
            line_part(bufs[a].at[d], h),
            z_ss.at[a, h, 0, side],
            z_rs.at[a, h, d],
            (other, e, t),
        )

    def z_hand(a, p, h):
        ref = line_part(bufs[a].at[blocks[p]], h)
        other = jnp.where(from_left[p] == 1, jnp.minimum(d + 1, last), jnp.maximum(d - 1, 0))
        return remote(ref, ref, z_ss.at[a, h, p, 0], z_rs.at[a, h, blocks[p]], (other, e, t))

    def z_goes_on(p):
        return jnp.where(from_left[p] == 1, d < last, d > 0)

    side_open = (d < last, d > 0)

    def send_own(a, h):
        for side in range(2):
            copy = z_own(a, h, side)

            @pl.when(side_open[side])
            def _(copy=copy):
                copy.start()

    def plane_copy(a, p, h, side, quarter_id):
        ref = bufs[a].at[blocks[p], quarter_id, :, pl.ds(h * piece, piece)]
        return remote(
            ref, ref, p_ss.at[a, p - 1, h, side], p_rs.at[a, p - 1, h, side],
            at_exp((x_id, y_id)[side]),
        )

    def relay_copy(a, p, h, side, quarter_id):
        ref = bufs[a].at[
            blocks[p], quarter_id, pl.ds((1 - side) * half, half), pl.ds(h * piece, piece)
        ]
        return remote(
            ref, ref, r_ss.at[a, p - 1, h, side], r_rs.at[a, p - 1, h, side],
            at_exp((x_id, y_id)[side]),
        )

    for h in range(n_pieces):
        send_own(0, h)
    for copy in idx_load:
        copy.wait()
    for k in shifts:
        for which in range(2):
            idx_copy(k, which).start()
    in_load[1].start()
    gw_load.start()
    uw_load.start()
    dw_load.start()

    def hop_line(a, p, h):
        hand = z_hand(a, p, h)
        hand.wait_recv()

        @pl.when(z_goes_on(p))
        def _():
            hand.start()

    def hop_plane(a, p, h):
        plane_copy(a, p, h, 0, e).start()
        plane_copy(a, p, h, 1, e).start()

    def hop_relay(a, p, h):
        plane_copy(a, p, h, 0, x_id).wait_recv()
        relay_copy(a, p, h, 1, x_id).start()
        plane_copy(a, p, h, 1, y_id).wait_recv()
        relay_copy(a, p, h, 0, y_id).start()

    def hop_last(a, p, h):
        relay_copy(a, p, h, 0, far).wait_recv()
        relay_copy(a, p, h, 1, far).wait_recv()

    def to_slots(a, p):
        lanes = width // split_count(width, 6)

        def body(i, carry):
            cols = pl.ds(pl.multiple_of(i * lanes, LANES), lanes)
            values = bufs[a][blocks[p], :, :, cols].reshape(rows, lanes)
            slots[a][pl.ds(p * CAP, CAP), cols] = dot_nn(sel[p, :CAP], values).astype(BF16)
            return carry

        lax.fori_loop(0, width // lanes, body, 0)

    def hits(p, k, count):
        pos = lax.broadcasted_iota(jnp.int32, (count, rows), 0)
        b = blocks[p]
        return (pick[b, k : k + 1] == e) & (place[b, k : k + 1] == pos)

    def make_select(p):
        hot = jnp.where(hits(p, 0, LANES) | hits(p, 1, LANES), 1.0, 0.0).astype(F32)
        sel[p] = hot.astype(BF16)
        selt[p] = hot.T.astype(BF16)

    def part_copy(which, j, k):
        cols = pl.ds(j * fc, fc)
        return remote(
            own.at[which, :, cols],
            peer.at[k - 1, which, :, cols],
            t_ss.at[k - 1, which, j],
            t_rs.at[k - 1, which, j],
            at_ten(k),
        )

    def part_tile(which, j, i):
        sub = pl.ds(pl.multiple_of(j * fc + i * f_tile, LANES), f_tile)
        if which < 2:
            value = dot_nn(st[...], (gw, uw)[which][:, sub])
        else:
            value = dot_nt(sg[...], dw[sub])
        own[which, :, sub] = value.astype(BF16)

    def send_part(which, j):
        for k in range(1, n_ten):
            part_copy(which, j, k).start()

    def part_matmul(which, j):
        def body(i, carry):
            part_tile(which, j, i)
            return carry

        lax.fori_loop(0, fc // f_tile, body, 0)
        send_part(which, j)

    def logits_of(p):
        logit_own[p] = dot_nt(rw[...], tok[blocks[p]].reshape(rows, width))

    def logit_copy(k):
        return remote(
            logit_own, logit_peer.at[k - 1], lg_ss.at[k - 1], lg_rs.at[k - 1], at_ten(k)
        )

    choice = lax.broadcasted_iota(jnp.int32, (n_choice, rows), 0)

    def routing():
        for m in range(1, n_ten):
            logit_copy(m).wait()
        for p in range(n_dp):
            logits = logit_own[p]
            for m in range(1, n_ten):
                logits = logits + logit_peer[m - 1, p]
            b = blocks[p]
            chosen = [
                jnp.sum(jnp.where(choice == pick[b, k : k + 1], logits, 0.0), axis=0, keepdims=True)
                for k in range(2)
            ]
            p0 = sigmoid(chosen[0] - chosen[1])
            p1 = sigmoid(chosen[1] - chosen[0])
            prob[p, 0:1] = p0
            prob[p, 1:2] = p1
            low0 = p0.astype(BF16).astype(F32)
            low1 = p1.astype(BF16).astype(F32)
            picked = jnp.where(hits(p, 0, CAP), low0, 0.0) + jnp.where(hits(p, 1, CAP), low1, 0.0)
            column = jnp.sum(picked, axis=1, keepdims=True)
            spb[pl.ds(p * CAP, CAP)] = jnp.broadcast_to(column, (CAP, LANES))
        dacc[...] = jnp.zeros_like(dacc)

    def mix_block(p, cols):
        base = pl.ds(p * CAP, CAP)
        total = []
        for which in range(3):
            value = own[which, base, cols].astype(F32)
            for k in range(1, n_ten):
                value = value + peer[k - 1, which, base, cols].astype(F32)
            total.append(value)
        g, u, ga = total
        s = sigmoid(g)
        gs = g * s
        hid = (gs * u).astype(BF16)
        dacc[base] = dacc[base] + hid.astype(F32) * ga
        act = spb[base] * ga
        own[0, base, cols] = hid
        own[1, base, cols] = (act * u * s * (1.0 + g * (1.0 - s))).astype(BF16)
        own[2, base, cols] = (act * gs).astype(BF16)

    def mix_wait(j):
        for which in range(3):
            for k in range(1, n_ten):
                part_copy(which, j, k).wait()

    def mix_tile(j, i):
        for q in range(f_tile // LANES):
            cols = pl.ds(pl.multiple_of(j * fc + i * f_tile + q * LANES, LANES), LANES)
            for p in range(n_dp):
                mix_block(p, cols)

    def mix(j):
        mix_wait(j)

        def body(i, carry):
            mix_tile(j, i)
            return carry

        lax.fori_loop(0, fc // f_tile, body, 0)

    pairs = [range(p, min(p + 2, n_dp)) for p in range(1, n_dp, 2)]
    orders = [[(a, p, h) for pair in pairs for h in range(splits) for p in pair] for a in range(2)]
    order = orders[0] + orders[1]
    beyond = [[(a, p, splits) for p in range(1, n_dp)] if extra else [] for a in range(2)]
    events = []
    for i, (a, p, h) in enumerate(order):
        lag = LAGS[a]
        ahead = LEADS[a] if i else 0
        events.append((i - ahead, 0, hop_line, (a, p, h)))
        events.append((i, 1, hop_plane, (a, p, h)))
        events.append((i + lag, 2, hop_relay, (a, p, h)))
        events.append((i + 2 * lag, 3, hop_last, (a, p, h)))
    for a in range(2):
        for i, which in enumerate(beyond[a]):
            time = len(orders[0]) * (a + 1) - len(beyond[a]) + i
            events.append((time + 0.5, 4, hop_line, which))
    events.sort(key=lambda event: event[:2])
    work = []
    left = [set(orders[a] + beyond[a]) for a in range(2)]
    events_left = len(events)
    tokens_done = False
    for position, (_, _, hop, which) in enumerate(events):
        hop(*which)
        events_left -= 1
        if position == EARLY_EVENTS:
            make_select(0)
            rw_load.wait()
            in_load[0].wait()
            to_slots(0, 0)
            logits_of(0)
        if hop is hop_line:
            if which == order[len(pairs[0]) - 1]:
                for h in range(n_pieces):
                    send_own(1, h)
        if hop is hop_last or which[2] == splits:
            a, p, h = which
            left[a].discard(which)
            if not any(other[1] == p for other in left[a]):
                if a == 0:
                    for kind in range(2):
                        idx_arrival(p, kind).wait_recv()
                    make_select(p)
                    logits_of(p)
                to_slots(a, p)
            if a == 0 and not left[0]:
                for m in range(1, n_ten):
                    logit_copy(m).start()
                in_load[1].wait()
                to_slots(1, 0)
                gw_load.wait()
                uw_load.wait()
                work += [functools.partial(part_matmul, w, j) for w in range(2) for j in range(f_chunks)]
                work.append(routing)
                tokens_done = True
        if tokens_done and work and hop in (hop_plane, hop_relay, hop_last):
            work.pop(0)()
    for job in work:
        job()
    dw_load.wait()

    for k in shifts:
        for which in range(2):
            idx_copy(k, which).wait_send()
    for a in range(2):
        for h in range(n_pieces):
            for side in range(2):
                copy = z_own(a, h, side)

                @pl.when(side_open[side])
                def _(copy=copy):
                    copy.wait_send()

    for a, p, h in order + beyond[0] + beyond[1]:
        hand = z_hand(a, p, h)

        @pl.when(z_goes_on(p))
        def _(hand=hand):
            hand.wait_send()

    for a, p, h in order:
        for side in range(2):
            plane_copy(a, p, h, side, e).wait_send()
            relay_copy(a, p, h, 1 - side, (x_id, y_id)[side]).wait_send()
    for j in range(f_chunks + 1):
        if j < f_chunks:
            part_matmul(2, j)
        if j >= 1:
            mix(j - 1)

    st_store = load(st, st_out, out_sem.at[3])
    st_store.start()
    own_store = [
        load(own.at[w], (None, gg_out, gu_out)[w], out_sem.at[w]) for w in (1, 2)
    ]
    for copy in own_store:
        copy.start()

    def router_zero():
        for p in range(n_dp):
            column = jnp.sum(dacc[pl.ds(p * CAP, CAP)], axis=1, keepdims=True)
            for k in range(2):
                dsend[blocks[p], k : k + 1] = jnp.sum(
                    jnp.where(hits(p, k, CAP), column, 0.0), axis=0, keepdims=True
                )
        for k in shifts:
            dz_copy(k).start()

    def dz_copy(k):
        return remote(dsend, dz.at[k - 1], dz_ss.at[k - 1], dz_rs.at[k - 1], at_dp(k))

    def de_copy(side):
        return remote(
            (d1, d2)[side], (dx1, dx2)[side], de_ss.at[side], de_rs.at[side],
            at_exp((x_id, y_id)[side]),
        )

    def scale_grads():
        lanes = width // split_count(width, 6)

        def body(i, carry):
            cols = pl.ds(pl.multiple_of(i * lanes, LANES), lanes)
            for p in range(n_dp):
                base = pl.ds(p * CAP, CAP)
                sg[base, cols] = (spb[base][:, 0:1] * sg[base, cols].astype(F32)).astype(BF16)
            return carry

        lax.fori_loop(0, width // lanes, body, 0)

    def router_one():
        total = dsend[...]
        for k in shifts:
            dz_copy(k).wait()
        for k in shifts:
            total = total + dz[k - 1]
        d1[...] = total
        de_copy(0).start()

    def router_two():
        de_copy(0).wait()
        d2[...] = d1[...] + dx1[...]
        de_copy(1).start()

    lanes = width // split_count(width, 6)

    def router_three():
        de_copy(1).wait()
        dx2[...] = d2[...] + dx2[...]
        for p in range(n_dp):
            b = blocks[p]
            g0, g1 = dx2[b, 0:1], dx2[b, 1:2]
            p0, p1 = prob[p, 0:1], prob[p, 1:2]
            mixed = p0 * g0 + p1 * g1
            w0, w1 = p0 * (g0 - mixed), p1 * (g1 - mixed)
            lg = jnp.where(choice == pick[b, 0:1], w0, 0.0) + jnp.where(
                choice == pick[b, 1:2], w1, 0.0
            )
            for i, part in enumerate(three_pieces(lg)):
                lgr[p, pl.ds(n_choice * i, n_choice)] = part
        weights = jnp.concatenate([rw[...].astype(F32)] * 3, axis=0).astype(BF16)

        def body(i, carry):
            cols = pl.ds(pl.multiple_of(i * lanes, LANES), lanes)
            out = jnp.zeros((3 * n_choice, lanes), F32)
            for p in range(n_dp):
                values = tok[blocks[p], :, :, cols].reshape(rows, lanes)
                out = out + dot_nn(lgr[p].astype(BF16), values)
            rgt[:, cols] = (
                out[0:n_choice] + out[n_choice : 2 * n_choice] + out[2 * n_choice : 3 * n_choice]
            )
            return carry

        lax.fori_loop(0, width // lanes, body, 0)
        term[...] = jnp.zeros_like(term)
        term[pl.ds(0, 3 * n_choice)] = lgr[0]
        term[...] = term[...].T
        mine = term[pl.ds(pl.multiple_of(e * quarter, 8), quarter)][:, : 3 * n_choice].astype(BF16)
        for i in range(width // lanes):
            cols = slice(i * lanes, (i + 1) * lanes)
            acc[:, cols] = dot_nn(mine, weights[:, cols])

    def dx_chunk(c):
        tile = wc // split_count(wc, 3)

        def body(i, carry):
            cols = pl.ds(pl.multiple_of(c * wc + i * tile, LANES), tile)
            part = dot_nt(own[1], gw[cols]) + dot_nt(own[2], uw[cols])
            part = part.astype(BF16)
            for p in range(n_dp):
                one = dot_nn(selt[p][:, :CAP], part[p * CAP : (p + 1) * CAP]).astype(BF16)
                tdx[p, :, :, cols] = one.reshape(n_exp, quarter, tile)
            return carry

        lax.fori_loop(0, wc // tile, body, 0)

    def a_copy(c, side, which):
        cols = pl.ds(c * wc, wc)
        quarter_id = ((x_id, far), (y_id, far))[side][which]
        return remote(
            tdx.at[:, quarter_id, pl.ds(side * half, half), cols],
            (ax, ay)[side].at[which, :, :, cols],
            a_ss.at[c, side, which],
            a_rs.at[c, side, which],
            at_exp((x_id, y_id)[side]),
        )

    def b_copy(c, side):
        cols = pl.ds(c * wc, wc)
        return remote(
            bsend.at[side, :, :, cols],
            brecv.at[side, :, :, cols],
            b_ss.at[c, side],
            b_rs.at[c, side],
            at_exp((y_id, x_id)[side]),
        )

    def c_copy(c, p):
        cols = pl.ds(c * wc, wc)
        return remote(
            csend.at[p, :, cols],
            crecv.at[d, :, cols],
            c_ss.at[c, p - 1],
            c_rs.at[c, d],
            (blocks[p], e, t),
        )

    def c_arrival(c, p):
        cols = pl.ds(c * wc, wc)
        return remote(
            csend.at[p, :, cols],
            crecv.at[blocks[p], :, cols],
            c_ss.at[c, p - 1],
            c_rs.at[c, blocks[p]],
            (blocks[p], e, t),
        )

    def start_a(c):
        for which in (1, 0):
            for side in range(2):
                a_copy(c, side, which).start()

    def relay_b(c):
        cols = pl.ds(c * wc, wc)
        for side in range(2):
            a_copy(c, side, 1).wait()
            mine = tdx[:, (y_id, x_id)[side], pl.ds(side * half, half), cols].astype(F32)
            got = (ax, ay)[side][1, :, :, cols].astype(F32)
            bsend[side, :, :, cols] = (mine + got).astype(BF16)
            b_copy(c, side).start()

    def cross_c(c):
        cols = pl.ds(c * wc, wc)
        for side in range(2):
            a_copy(c, side, 0).wait()
            b_copy(c, side).wait()
            part = pl.ds(side * half, half)
            total = tdx[:, e, part, cols].astype(F32)
            total = total + (ax, ay)[side][0, :, :, cols].astype(F32)
            total = total + brecv[side, :, :, cols].astype(F32)
            csend[:, part, cols] = total.astype(BF16)
        for p in range(1, n_dp):
            c_copy(c, p).start()

    def finish(c):
        cols = pl.ds(c * wc, wc)
        total = csend[0, :, cols].astype(F32)
        for p in range(1, n_dp):
            c_copy(c, p).wait_send()
            c_arrival(c, p).wait_recv()
        for p in range(1, n_dp):
            total = total + crecv[blocks[p], :, cols].astype(F32)
        csend[0, :, cols] = (acc[:, cols] + total).astype(BF16)

    dg_rows = hidden_w // dg_chunks
    dg_store = [
        load(dw.at[pl.ds(i * dg_rows, dg_rows)], dg_out.at[pl.ds(i * dg_rows, dg_rows)], dg_sem.at[i])
        for i in range(dg_chunks)
    ]

    def down_grad(i):
        lhs = own[0, :, pl.ds(i * dg_rows, dg_rows)].astype(F32).T.astype(BF16)

        def body(k, carry):
            cols = pl.ds(pl.multiple_of(k * lanes, LANES), lanes)
            dw[pl.ds(i * dg_rows, dg_rows), cols] = dot_nn(lhs, sg[:, cols]).astype(BF16)
            return carry

        lax.fori_loop(0, width // lanes, body, 0)
        dg_store[i].start()

    small = {0: [router_zero], 1: [scale_grads], 3: [router_one], w_chunks: [router_two]}
    fill = [functools.partial(down_grad, i) for i in range(dg_chunks)]

    for c in range(w_chunks + 2):
        if c < w_chunks:
            dx_chunk(c)
            start_a(c)
        elif fill:
            fill.pop(0)()
        for job in small.pop(c, []):
            job()
        if 0 <= c - 2 < w_chunks:
            relay_b(c - 2)
        if 0 <= c - 4 < w_chunks:
            cross_c(c - 4)
    for jobs in small.values():
        for job in jobs:
            job()
    if fill:
        fill.pop(0)()
    for c in range(max(w_chunks - 2, 0), w_chunks):
        cross_c(c)
    router_three()
    for job in fill:
        job()
    rg_store = load(rgt, rg_out, out_sem.at[6])
    rg_store.start()
    for c in range(w_chunks):
        finish(c)

    dx_store = load(csend.at[0], dx_out, out_sem.at[5])
    dx_store.start()
    st_store.wait()
    for copy in own_store:
        copy.wait()
    for copy in dg_store:
        copy.wait()
    dx_store.wait()
    rg_store.wait()


def run_kernel(
    n_dp, n_exp, n_ten, tokens, out_grad, router, chosen, place, gate_w, up_w, down_w
):
    rows, width = tokens.shape
    hidden_w = gate_w.shape[1]
    quarter = rows // n_exp
    half = quarter // 2
    slots = n_dp * CAP
    f_chunks = split_count(hidden_w, 4)
    w_chunks = split_count(width, 6)
    splits = split_count(width - spare_columns(width), 2)
    pieces = splits + 1
    dg_chunks = split_count(hidden_w, 4)
    n_choice = router.shape[0]
    shape = jax.ShapeDtypeStruct
    any_spec = pl.BlockSpec(memory_space=pl.ANY)
    dma = pltpu.SemaphoreType.DMA
    vmem = pltpu.VMEM
    z = n_dp - 1
    m = max(n_ten - 1, 1)
    scratch = [
        vmem((width, hidden_w), BF16),
        vmem((width, hidden_w), BF16),
        vmem((hidden_w, width), BF16),
        vmem((n_dp, n_exp, quarter, width), BF16),
        vmem((n_dp, n_exp, quarter, width), BF16),
        vmem((slots, width), BF16),
        vmem((slots, width), BF16),
        vmem((3, slots, hidden_w), BF16),
        vmem((m, 3, slots, hidden_w), BF16),
        vmem((2, n_dp, half, width), BF16),
        vmem((2, n_dp, half, width), BF16),
        vmem((2, n_dp, half, width), BF16),
        vmem((2, n_dp, half, width), BF16),
        vmem((n_dp, quarter, width), BF16),
        vmem((n_dp, quarter, width), BF16),
        vmem((quarter, width), F32),
        vmem((n_dp, 2, rows), jnp.int32),
        vmem((n_dp, 2, rows), jnp.int32),
        vmem((n_choice, width), BF16),
        vmem((n_dp, n_choice, rows), F32),
        vmem((m, n_dp, n_choice, rows), F32),
        vmem((n_dp, 2, rows), F32),
        vmem((n_dp, LANES, rows), BF16),
        vmem((n_dp, rows, LANES), BF16),
        vmem((slots, LANES), F32),
        vmem((slots, LANES), F32),
        vmem((n_dp, 2, rows), F32),
        vmem((z, n_dp, 2, rows), F32),
        vmem((n_dp, 2, rows), F32),
        vmem((n_dp, 2, rows), F32),
        vmem((n_dp, 2, rows), F32),
        vmem((n_dp, 2, rows), F32),
        vmem((n_dp, 3 * n_choice, rows), F32),
        vmem((rows, rows), F32),
        vmem((n_choice, width), F32),
        dma((6,)),
        dma((2,)),
        dma((2, z)), dma((2, n_dp)),
        dma((2, pieces, n_dp, 2)), dma((2, pieces, n_dp)),
        dma((2, z, splits, 2)), dma((2, z, splits, 2)),
        dma((2, z, splits, 2)), dma((2, z, splits, 2)),
        dma((m, 3, f_chunks)), dma((m, 3, f_chunks)),
        dma((m,)), dma((m,)),
        dma((w_chunks, 2, 2)), dma((w_chunks, 2, 2)),
        dma((w_chunks, 2)), dma((w_chunks, 2)),
        dma((w_chunks, z)), dma((w_chunks, n_dp)),
        dma((z,)), dma((z,)),
        dma((2,)), dma((2,)),
        dma((7,)),
        dma((dg_chunks,)),
    ]
    flops = 2 * slots * width * hidden_w * 5
    return pl.pallas_call(
        functools.partial(layer_kernel, n_dp, n_exp, n_ten, f_chunks, w_chunks, splits, dg_chunks),
        out_shape=(
            shape((slots, hidden_w), BF16),
            shape((slots, hidden_w), BF16),
            shape((slots, width), BF16),
            shape((hidden_w, width), BF16),
            shape((quarter, width), BF16),
            shape((n_choice, width), F32),
        ),
        in_specs=[any_spec] * 8,
        out_specs=(any_spec,) * 6,
        scratch_shapes=scratch,
        compiler_params=pltpu.CompilerParams(
            collective_id=0, has_side_effects=True, vmem_limit_bytes=VMEM_LIMIT
        ),
        cost_estimate=pl.CostEstimate(
            flops=flops, bytes_accessed=6 * width * hidden_w, transcendentals=0
        ),
        name="layer",
    )(
        tokens.reshape(n_exp, quarter, width),
        out_grad.reshape(n_exp, quarter, width),
        router, chosen, place, gate_w, up_w, down_w,
    )


def weight_grads(slot_tokens, grad_gate, grad_up, down):
    slots, width = slot_tokens.shape
    hidden_w = grad_gate.shape[1]
    steps = max(s for s in range(1, 9) if width % (s * LANES) == 0 and hidden_w % (16 * s) == 0)
    tile = width // steps

    def body(st, gg, gu, down_in, gate_out, up_out, down_out):
        lhs = st[...]
        gate_out[...] = dot_tn(lhs, gg[...]).astype(BF16)
        up_out[...] = dot_tn(lhs, gu[...]).astype(BF16)
        down_out[...] = down_in[...]

    whole = pl.BlockSpec((slots, hidden_w), lambda i: (0, 0))
    by_rows = pl.BlockSpec((tile, hidden_w), lambda i: (i, 0))
    down_rows = pl.BlockSpec((hidden_w // steps, width), lambda i: (i, 0))
    shape = jax.ShapeDtypeStruct((width, hidden_w), BF16)
    return pl.pallas_call(
        body,
        grid=(steps,),
        out_shape=(shape, shape, jax.ShapeDtypeStruct((hidden_w, width), BF16)),
        in_specs=[pl.BlockSpec((slots, tile), lambda i: (0, i)), whole, whole, down_rows],
        out_specs=(by_rows, by_rows, down_rows),
        compiler_params=pltpu.CompilerParams(
            dimension_semantics=("arbitrary",), vmem_limit_bytes=VMEM_LIMIT - 2**20
        ),
        cost_estimate=pl.CostEstimate(
            flops=4 * slots * width * hidden_w, bytes_accessed=8 * width * hidden_w, transcendentals=0
        ),
        name="weight_grads",
    )(slot_tokens, grad_gate, grad_up, down)


def build(n_dp, n_exp, n_ten):
    def shards(
        tokens, out_grad, router_weight, gate_weight, up_weight, down_weight, expert_index, slot_index
    ):
        grad_gate, grad_up, slot_tokens, down, tokens_grad, router_t = run_kernel(
            n_dp, n_exp, n_ten, tokens, out_grad, router_weight.T, expert_index.T, slot_index.T,
            gate_weight[0], up_weight[0], down_weight[0],
        )
        gate_grad, up_grad, down_grad = weight_grads(slot_tokens, grad_gate, grad_up, down)
        router_grad = router_t.T
        return (tokens_grad, router_grad, gate_grad[None], up_grad[None], down_grad[None])

    return shards


def solution(mesh):
    in_specs = (
        P("dp", "tensor"),
        P("dp", "tensor"),
        P("tensor", None),
        P("expert", "tensor", "dp"),
        P("expert", "tensor", "dp"),
        P("expert", "dp", "tensor"),
        P("dp", None),
        P("dp", None),
    )
    out_specs = (
        P(("dp", "expert"), "tensor"),
        P("tensor", None),
        P("expert", "tensor", "dp"),
        P("expert", "tensor", "dp"),
        P("expert", "dp", "tensor"),
    )
    shards = build(mesh.shape["dp"], mesh.shape["expert"], mesh.shape["tensor"])
    return jax.shard_map(shards, mesh=mesh, in_specs=in_specs, out_specs=out_specs, check_vma=False)
```

time: 155 us -> 137 us (0.88)
  matrix products: 30.9 us -> 0 us
  Pallas kernels: 118 us -> 135 us
  local copies, waits for them, and re-layouts: 4.18 us -> 1.31 us
    dot_general x3 -> x0, matrix products: 30.9 us -> none  [dot_tn(): lax.dot_general(a, b, (((0,), (0,)), ((), ())), preferred_element_type=F32)]
    pallas_call x0 -> x1, Pallas kernels: none -> 22.3 us  [weight_grads(): pl.pallas_call(body, grid=(steps,), out_shape=(shape, shape, jax.ShapeDty...]
    pallas_call x1, Pallas kernels: 118 us -> 112 us  [run_kernel(): pl.pallas_call(functools.partial(layer_kernel, n_dp, n_exp, n_ten, f_chun...]
    pad x2 -> x0, local copies, waits for them, and re-layouts: 1.97 us -> none  [the longest x1 1.37 us: run_kernel(): router = jnp.pad(router_weight.T, ((0, 8 - n_choice), (0, 0)))]
where the time goes in v1:
time: 137 us
  Pallas kernels  135 us (99%)
    pallas_call x1, Pallas kernels, run_kernel(): pl.pallas_call(functools.partial(layer_kernel, n_dp, n_exp, n_ten, f_chun...  112 us
    pallas_call x1, Pallas kernels, weight_grads(): pl.pallas_call(body, grid=(steps,), out_shape=(shape, shape, jax.ShapeDty...  22.3 us

profile of v1, /device:TPU:0, one launch (start us, length us, event | category | flops | bytes accessed | tf_op | source)
XLA Modules:
  0.0 136.7 jit_solution(17565958548737915617)
XLA Ops:
  0.6 112.4 %layer.1 = (bf16[384,2048]{1,0:T(8,128)(2,1)}, bf16[384,2048]{1,0:T(8,128)(2,1)}, bf16[384,3072]{1,0:T(8,128)(2,1)}, bf16[2048,3072]{1,0:T(8,128)(2,1)}, bf16[32,3072]{1,0:T(8,128)(2,1)}, /*index=5*/f32[4,3072]{1,0:T(4,128)}) custom-call(bf16[4,32,3072]{2,1,0:T(8,128)(2,1)} %bitcast.16, bf16[4,32,3072]{2,1,0:T(8,128)(2,1)} %bitcast.17, ...), custom_call_target="tpu_custom_call" | custom-call | flops 24159191040 | bytes 37748736 | tf_op jit(solution)/shard_map/layer/pallas_call | solution.py:748
  113.0 0.0 copy-start
  113.0 0.0 copy-start.1
  113.0 22.3 %weight_grads.1 = (bf16[3072,2048]{1,0:T(8,128)(2,1)}, bf16[3072,2048]{1,0:T(8,128)(2,1)}, bf16[2048,3072]{1,0:T(8,128)(2,1)}) custom-call(bf16[384,3072]{1,0:T(8,128)(2,1)} %get-tuple-element.16.st, bf16[384,2048]{1,0:T(8,128)(2,1)} %get-tuple-element.17.gg, bf16[384,2048]{1,0:T(8,128)(2,1)} %get-tuple-element.18.gu, ...), custom_call_target="tpu_custom_call" | custom-call | flops 9663676416 | bytes 50331648 | tf_op jit(solution)/shard_map/weight_grads/pallas_call | solution.py:791
  135.4 0.0 copy-done
  135.4 0.7 copy.15
  136.0 0.0 copy-done.1
  136.0 0.6 copy.16
Async XLA Ops:
  113.0 22.3 %copy-start = (bf16[32,3072]{1,0:T(8,128)(2,1)S(1)}, bf16[32,3072]{1,0:T(8,128)(2,1)}, u32[]{:S(2)}) copy-start(bf16[32,3072]{1,0:T(8,128)(2,1)} %get-tuple-element.28) | copy-start | bytes 589828
  113.0 23.0 %copy-start.1 = (f32[4,3072]{1,0:T(4,128)S(1)}, f32[4,3072]{1,0:T(4,128)}, u32[]{:S(2)}) copy-start(f32[4,3072]{1,0:T(4,128)} %get-tuple-element.15) | copy-start | bytes 147460

commit v2 on v1

--- a/solution.py
+++ b/solution.py
@@ -9,6 +9,7 @@
 
 CAP = 96
 LAGS = (1, 2)
+OWN_AFTER = 1
 LEADS = (0.5, 1.5)
 EARLY_EVENTS = 3
 F32 = jnp.float32
@@ -48,12 +49,20 @@
     return 1
 
 
+def column_chunks(width):
+    if width % (12 * LANES) == 0:
+        sizes = [width // 12] + [width // 6] * 5 + [width // 12]
+    else:
+        sizes = [width // split_count(width, 6)] * split_count(width, 6)
+    return [(sum(sizes[:i]), sizes[i]) for i in range(len(sizes))]
+
+
 def spare_columns(width):
     return width // 12 if width % (12 * LANES) == 0 else 0
 
 
 def layer_kernel(
-    n_dp, n_exp, n_ten, f_chunks, w_chunks, splits, dg_chunks,
+    n_dp, n_exp, n_ten, f_chunks, splits, dg_chunks,
     tokens, out_grad, router, chosen_in, place_in, gate_w, up_w, down_w,
     gg_out, gu_out, st_out, dg_out, dx_out, rg_out,
     gw, uw, dw, tok, gra, st, sg, own, peer, ax, ay, bsend, brecv, csend, crecv, acc,
@@ -71,7 +80,8 @@
     n_choice = rw.shape[0]
     hidden_w = gw.shape[1]
     fc = hidden_w // f_chunks
-    wc = width // w_chunks
+    chunks = column_chunks(width)
+    w_chunks = len(chunks)
     extra = spare_columns(width)
     piece = (width - extra) // splits
     n_pieces = splits + (1 if extra else 0)
@@ -186,7 +196,7 @@
             at_exp((x_id, y_id)[side]),
         )
 
-    for h in range(n_pieces):
+    for h in range(splits):
         send_own(0, h)
     for copy in idx_load:
         copy.wait()
@@ -374,6 +384,9 @@
             logits_of(0)
         if hop is hop_line:
             if which == order[len(pairs[0]) - 1]:
+                for h in range(splits, n_pieces):
+                    send_own(0, h)
+            if which == orders[0][OWN_AFTER]:
                 for h in range(n_pieces):
                     send_own(1, h)
         if hop is hop_last or which[2] == splits:
@@ -523,10 +536,11 @@
             acc[:, cols] = dot_nn(mine, weights[:, cols])
 
     def dx_chunk(c):
-        tile = wc // split_count(wc, 3)
+        first, size = chunks[c]
+        tile = min(size, 2 * LANES)
 
         def body(i, carry):
-            cols = pl.ds(pl.multiple_of(c * wc + i * tile, LANES), tile)
+            cols = pl.ds(pl.multiple_of(first + i * tile, LANES), tile)
             part = dot_nt(own[1], gw[cols]) + dot_nt(own[2], uw[cols])
             part = part.astype(BF16)
             for p in range(n_dp):
@@ -534,10 +548,10 @@
                 tdx[p, :, :, cols] = one.reshape(n_exp, quarter, tile)
             return carry
 
-        lax.fori_loop(0, wc // tile, body, 0)
+        lax.fori_loop(0, size // tile, body, 0)
 
     def a_copy(c, side, which):
-        cols = pl.ds(c * wc, wc)
+        cols = pl.ds(*chunks[c])
         quarter_id = ((x_id, far), (y_id, far))[side][which]
         return remote(
             tdx.at[:, quarter_id, pl.ds(side * half, half), cols],
@@ -548,7 +562,7 @@
         )
 
     def b_copy(c, side):
-        cols = pl.ds(c * wc, wc)
+        cols = pl.ds(*chunks[c])
         return remote(
             bsend.at[side, :, :, cols],
             brecv.at[side, :, :, cols],
@@ -558,7 +572,7 @@
         )
 
     def c_copy(c, p):
-        cols = pl.ds(c * wc, wc)
+        cols = pl.ds(*chunks[c])
         return remote(
             csend.at[p, :, cols],
             crecv.at[d, :, cols],
@@ -568,7 +582,7 @@
         )
 
     def c_arrival(c, p):
-        cols = pl.ds(c * wc, wc)
+        cols = pl.ds(*chunks[c])
         return remote(
             csend.at[p, :, cols],
             crecv.at[blocks[p], :, cols],
@@ -583,7 +597,7 @@
                 a_copy(c, side, which).start()
 
     def relay_b(c):
-        cols = pl.ds(c * wc, wc)
+        cols = pl.ds(*chunks[c])
         for side in range(2):
             a_copy(c, side, 1).wait()
             mine = tdx[:, (y_id, x_id)[side], pl.ds(side * half, half), cols].astype(F32)
@@ -592,7 +606,7 @@
             b_copy(c, side).start()
 
     def cross_c(c):
-        cols = pl.ds(c * wc, wc)
+        cols = pl.ds(*chunks[c])
         for side in range(2):
             a_copy(c, side, 0).wait()
             b_copy(c, side).wait()
@@ -605,7 +619,7 @@
             c_copy(c, p).start()
 
     def finish(c):
-        cols = pl.ds(c * wc, wc)
+        cols = pl.ds(*chunks[c])
         total = csend[0, :, cols].astype(F32)
         for p in range(1, n_dp):
             c_copy(c, p).wait_send()
@@ -620,15 +634,17 @@
         for i in range(dg_chunks)
     ]
 
+    dg_lanes = width // split_count(width, 3)
+
     def down_grad(i):
         lhs = own[0, :, pl.ds(i * dg_rows, dg_rows)].astype(F32).T.astype(BF16)
 
         def body(k, carry):
-            cols = pl.ds(pl.multiple_of(k * lanes, LANES), lanes)
+            cols = pl.ds(pl.multiple_of(k * dg_lanes, LANES), dg_lanes)
             dw[pl.ds(i * dg_rows, dg_rows), cols] = dot_nn(lhs, sg[:, cols]).astype(BF16)
             return carry
 
-        lax.fori_loop(0, width // lanes, body, 0)
+        lax.fori_loop(0, width // dg_lanes, body, 0)
         dg_store[i].start()
 
     small = {0: [router_zero], 1: [scale_grads], 3: [router_one], w_chunks: [router_two]}
@@ -681,7 +697,7 @@
     half = quarter // 2
     slots = n_dp * CAP
     f_chunks = split_count(hidden_w, 4)
-    w_chunks = split_count(width, 6)
+    w_chunks = len(column_chunks(width))
     splits = split_count(width - spare_columns(width), 2)
     pieces = splits + 1
     dg_chunks = split_count(hidden_w, 4)
@@ -746,7 +762,7 @@
     ]
     flops = 2 * slots * width * hidden_w * 5
     return pl.pallas_call(
-        functools.partial(layer_kernel, n_dp, n_exp, n_ten, f_chunks, w_chunks, splits, dg_chunks),
+        functools.partial(layer_kernel, n_dp, n_exp, n_ten, f_chunks, splits, dg_chunks),
         out_shape=(
             shape((slots, hidden_w), BF16),
             shape((slots, hidden_w), BF16),
@@ -775,7 +791,7 @@
 def weight_grads(slot_tokens, grad_gate, grad_up, down):
     slots, width = slot_tokens.shape
     hidden_w = grad_gate.shape[1]
-    steps = max(s for s in range(1, 9) if width % (s * LANES) == 0 and hidden_w % (16 * s) == 0)
+    steps = max(s for s in range(1, 5) if width % (s * LANES) == 0 and hidden_w % (16 * s) == 0)
     tile = width // steps
 
     def body(st, gg, gu, down_in, gate_out, up_out, down_out):

time: 137 us -> 136 us (level)
  Pallas kernels: 135 us -> 133 us
where the time goes in v2:
time: 136 us; the launch traced here: 135 us
  Pallas kernels  133 us (98%)
    pallas_call x1, Pallas kernels, run_kernel(): pl.pallas_call(functools.partial(layer_kernel, n_dp, n_exp, n_ten, f_chun...  112 us
    pallas_call x1, Pallas kernels, weight_grads(): pl.pallas_call(body, grid=(steps,), out_shape=(shape, shape, jax.ShapeDty...  21.5 us

profile of v2, /device:TPU:0, one launch (start us, length us, event | category | flops | bytes accessed | tf_op | source)
XLA Modules:
  0.0 135.4 jit_solution(13830171060889898683)
XLA Ops:
  0.6 111.9 %layer.1 = (bf16[384,2048]{1,0:T(8,128)(2,1)}, bf16[384,2048]{1,0:T(8,128)(2,1)}, bf16[384,3072]{1,0:T(8,128)(2,1)}, bf16[2048,3072]{1,0:T(8,128)(2,1)}, bf16[32,3072]{1,0:T(8,128)(2,1)}, /*index=5*/f32[4,3072]{1,0:T(4,128)}) custom-call(bf16[4,32,3072]{2,1,0:T(8,128)(2,1)} %bitcast.16, bf16[4,32,3072]{2,1,0:T(8,128)(2,1)} %bitcast.17, ...), custom_call_target="tpu_custom_call" | custom-call | flops 24159191040 | bytes 37748736 | tf_op jit(solution)/shard_map/layer/pallas_call | solution.py:764
  112.5 0.0 copy-start
  112.5 0.0 copy-start.1
  112.5 21.5 %weight_grads.1 = (bf16[3072,2048]{1,0:T(8,128)(2,1)}, bf16[3072,2048]{1,0:T(8,128)(2,1)}, bf16[2048,3072]{1,0:T(8,128)(2,1)}) custom-call(bf16[384,3072]{1,0:T(8,128)(2,1)} %get-tuple-element.16.st, bf16[384,2048]{1,0:T(8,128)(2,1)} %get-tuple-element.17.gg, bf16[384,2048]{1,0:T(8,128)(2,1)} %get-tuple-element.18.gu, ...), custom_call_target="tpu_custom_call" | custom-call | flops 9663676416 | bytes 50331648 | tf_op jit(solution)/shard_map/weight_grads/pallas_call | solution.py:807
  134.1 0.0 copy-done
  134.1 0.7 copy.15
  134.8 0.0 copy-done.1
  134.8 0.6 copy.16
Async XLA Ops:
  112.5 21.6 %copy-start = (bf16[32,3072]{1,0:T(8,128)(2,1)S(1)}, bf16[32,3072]{1,0:T(8,128)(2,1)}, u32[]{:S(2)}) copy-start(bf16[32,3072]{1,0:T(8,128)(2,1)} %get-tuple-element.28) | copy-start | bytes 589828
  112.5 22.2 %copy-start.1 = (f32[4,3072]{1,0:T(4,128)S(1)}, f32[4,3072]{1,0:T(4,128)}, u32[]{:S(2)}) copy-start(f32[4,3072]{1,0:T(4,128)} %get-tuple-element.15) | copy-start | bytes 147460
